TPU v7x, 32 devices: a whole 2x2x4 slice. The times are simulated.
32 devices in a mesh: section: 4 (over z), dp: 2 (over y), tensor: 4 (over x, core).
Axes of the slice: x: 2, y: 2, z: 4, core: 2. Of those that a mesh axis runs over, the one named last changes fastest.
Arguments:
- inputs: bfloat16 [8, 2, 64, 2560], P('dp', None, None, ('section', 'tensor')), parts along dimension 0, may hold values from -18 to 18
- sequence_jobs: int32 [8, 2, 1], P('dp'), parts along dimension 0, may hold values from 0 to 3
- entry_sequence: int32 [8], P('dp'), parts along dimension 0, may hold values from 0 to 3, each once
- layer_norm_gain: float32 [4, 2560], P('section'), may hold values from 0.25 to 1.75
- frozen_query_matrix: bfloat16 [4, 2560, 2560], P('section', None, 'tensor'), may hold values from -1 to 1
- frozen_key_matrix: bfloat16 [4, 2560, 2560], P('section', None, 'tensor'), may hold values from -24 to 24
- frozen_value_matrix: bfloat16 [4, 2560, 2560], P('section', None, 'tensor'), may hold values from -0.125 to 0.125
- frozen_output_matrix: bfloat16 [4, 2560, 2560], P('section', 'tensor'), may hold values from -0.125 to 0.125
- adapter_down_maps: bfloat16 [4, 2560, 128], P('section', 'tensor'), may hold values from -0.125 to 0.125
- adapter_up_maps: bfloat16 [4, 2, 64, 2560], P('section', None, None, 'tensor'), may hold values from -1.5 to 1.5
Outputs:
- finished: bfloat16 [8, 2, 64, 2560], P('dp', None, None, ('section', 'tensor')), parts along dimension 0
There are 2 independent parts, one for each index of `dp`. A program takes and returns all parts, laid end to end along the dimension named above; an argument that names none is the same for every part. Nothing has to cross between parts.
Inputs may be any that keep to these rules, and one draw needn't show every extreme that they name: `sequence_jobs`: every one of the 4 jobs owns at least one sequence. `entry_sequence`: a permutation of the 4 micro-batches.
All inputs are finite; a program needn't handle non-finite values.
Results may differ from a plain program's by a relative error of at most 0.039.
Values may be sent and summed in bfloat16 or wider, within the bound.
A program may use at most 64 MiB of HBM per device.

v0:
```python
import jax
import jax.numpy as jnp
from jax import lax
from jax.sharding import PartitionSpec as P

HEAD_DIM = 128
ADAPTER_RANK = 16
ADAPTER_JOBS = 4


adapter_scale = 2.0


def shifted(value, axis, steps):
    count = lax.axis_size(axis)
    leading, last = (max(0, -steps), min(count, count - steps))
    return lax.ppermute(value, axis, [(source, source + steps) for source in range(leading, last)])


def spread(array, axis, root):
    mine = lax.axis_index(axis) == root
    return lax.psum(jnp.where(mine, array, jnp.zeros_like(array)), axis)


def attend(query_rows, key_vecs, value_rows, head_groupings, sequence_length):
    head_count = query_rows.shape[1] // HEAD_DIM
    grid_shape = (head_groupings, sequence_length, head_count, HEAD_DIM)
    scores = jnp.einsum(
        "bqhd,bkhd->bhqk",
        query_rows.reshape(grid_shape),
        key_vecs.reshape(grid_shape),
        preferred_element_type=jnp.float32,
    ) * HEAD_DIM ** (-0.5)
    causal = lax.broadcasted_iota(
        jnp.int32, (sequence_length, sequence_length), 0
    ) >= lax.broadcasted_iota(jnp.int32, (sequence_length, sequence_length), 1)
    scores = jnp.where(causal, scores, -jnp.inf)
    row_max = jnp.max(scores, axis=-1, keepdims=True)
    weights = jnp.exp(scores - row_max)
    probabilities = (weights / jnp.sum(weights, axis=-1, keepdims=True)).astype(jnp.bfloat16)
    mixture = jnp.einsum(
        "bhqk,bkhd->bqhd",
        probabilities,
        value_rows.reshape(grid_shape),
        preferred_element_type=jnp.float32,
    )
    return mixture.astype(jnp.bfloat16).reshape(
        head_groupings * sequence_length, head_count * HEAD_DIM
    )


def prepare_inputs(
    complete_result, inverse_norm_scale, adapter_rows, partition_number, column_slice
):
    widened = complete_result.astype(jnp.float32)
    meansq = jnp.mean(widened * widened, axis=-1, keepdims=True)
    normalized_input = (widened * lax.rsqrt(meansq + 1e-05) * inverse_norm_scale).astype(
        jnp.bfloat16
    )
    local_normalized = lax.dynamic_slice_in_dim(
        normalized_input, partition_number * column_slice, column_slice, 1
    )
    return (
        normalized_input,
        jnp.dot(local_normalized, adapter_rows, preferred_element_type=jnp.float32),
    )


def final_output(
    normalized_input,
    lowrank_products,
    query_matrix,
    key_matrix,
    value_matrix,
    output_matrix,
    adapter_upper_part,
    head_groupings,
    sequence_length,
):
    middle_result = lowrank_products.shape[1] // 2
    query_rows = (
        jnp.dot(normalized_input, query_matrix, preferred_element_type=jnp.float32)
        + adapter_scale
        * jnp.dot(
            lowrank_products[:, :middle_result],
            adapter_upper_part[0],
            preferred_element_type=jnp.float32,
        )
    ).astype(jnp.bfloat16)
    key_vecs = jnp.dot(normalized_input, key_matrix, preferred_element_type=jnp.float32).astype(
        jnp.bfloat16
    )
    value_rows = (
        jnp.dot(normalized_input, value_matrix, preferred_element_type=jnp.float32)
        + adapter_scale
        * jnp.dot(
            lowrank_products[:, middle_result:],
            adapter_upper_part[1],
            preferred_element_type=jnp.float32,
        )
    ).astype(jnp.bfloat16)
    heads = attend(query_rows, key_vecs, value_rows, head_groupings, sequence_length)
    return (
        jnp.dot(heads, output_matrix, preferred_element_type=jnp.float32)
        .astype(jnp.bfloat16)
        .astype(jnp.float32)
    )


def shards(
    inputs,
    sequence_jobs,
    entry_sequence,
    layer_norm_gain,
    frozen_query_matrix,
    frozen_key_matrix,
    frozen_value_matrix,
    frozen_output_matrix,
    adapter_down_maps,
    adapter_up_maps,
):
    sections = lax.axis_size("section")
    across = lax.axis_size("tensor")
    section_id = lax.axis_index("section")
    partition_number = lax.axis_index("tensor")
    entire = lax.all_gather(inputs, ("section", "tensor"), axis=3, tiled=True)
    batches, head_groupings, sequence_length, features = entire.shape
    column_slice = frozen_query_matrix.shape[2]
    lowrank_width = adapter_down_maps.shape[2]
    tok_rows = head_groupings * sequence_length
    step_count = batches + sections - 1

    def compute(complete_result, step_idx):
        position = step_idx - section_id
        active = jnp.logical_and(position >= 0, position < batches)
        chosen = entry_sequence[jnp.clip(position, 0, batches - 1)]
        seq_jobs = lax.dynamic_index_in_dim(sequence_jobs, chosen, 0, keepdims=False)
        job_per_row = jnp.repeat(seq_jobs[:, 0], sequence_length)
        normalized_input, part_codes = lax.cond(
            active,
            lambda: prepare_inputs(
                complete_result,
                layer_norm_gain[0],
                adapter_down_maps[0],
                partition_number,
                column_slice,
            ),
            lambda: (
                jnp.zeros((tok_rows, features), jnp.bfloat16),
                jnp.zeros((tok_rows, lowrank_width), jnp.float32),
            ),
        )
        summed_codes = lax.psum(part_codes, "tensor")
        column_job = (
            lax.broadcasted_iota(jnp.int32, (lowrank_width,), 0) // ADAPTER_RANK % ADAPTER_JOBS
        )
        lowrank_products = jnp.where(
            column_job[None, :] == job_per_row[:, None], summed_codes, 0.0
        ).astype(jnp.bfloat16)
        return lax.cond(
            active,
            lambda: final_output(
                normalized_input,
                lowrank_products,
                frozen_query_matrix[0],
                frozen_key_matrix[0],
                frozen_value_matrix[0],
                frozen_output_matrix[0],
                adapter_up_maps[0],
                head_groupings,
                sequence_length,
            ),
            lambda: jnp.zeros((tok_rows, features), jnp.float32),
        )

    def injected(step_idx):
        chosen = entry_sequence[jnp.minimum(step_idx, batches - 1)]
        return lax.dynamic_index_in_dim(entire, chosen, 0, keepdims=False).reshape(
            tok_rows, features
        )

    def record(stored, step_idx, piece):
        out_slot = step_idx - (sections - 1)
        keeping = jnp.logical_and(section_id == sections - 1, out_slot >= 0)
        updated = lax.dynamic_update_index_in_dim(stored, piece, jnp.maximum(out_slot, 0), 0)
        return jnp.where(keeping, updated, stored)

    stored = jnp.zeros((batches, tok_rows, column_slice), jnp.bfloat16)

    def advance(step_idx, carried):
        arrived, stored = carried
        entering = lax.dynamic_slice_in_dim(
            injected(step_idx), partition_number * column_slice, column_slice, 1
        )
        owned = jnp.where(section_id == 0, entering, arrived)
        complete_result = lax.all_gather(owned, "tensor", axis=1, tiled=True)
        term = compute(complete_result, step_idx)
        share = lax.psum_scatter(
            term.astype(jnp.bfloat16), "tensor", scatter_dimension=1, tiled=True
        ).astype(jnp.float32)
        updated_x = (owned.astype(jnp.float32) + share).astype(jnp.bfloat16)
        stored = record(stored, step_idx, updated_x)
        arrived = shifted(updated_x, ("section", "tensor"), across)
        return (arrived, stored)

    initial = jnp.zeros((tok_rows, column_slice), jnp.bfloat16)
    arrived, stored = lax.fori_loop(0, step_count, advance, (initial, stored))
    result = spread(stored, "section", sections - 1)
    complete = lax.all_gather(result, "tensor", axis=2, tiled=True)
    width = features // (sections * across)
    piece = lax.dynamic_slice_in_dim(
        complete, (section_id * across + partition_number) * width, width, 2
    )
    return piece.reshape(batches, head_groupings, sequence_length, width)


def solution(mesh):
    in_specs = (
        P("dp", None, None, ("section", "tensor")),
        P("dp", None, None),
        P("dp"),
        P("section", None),
        P("section", None, "tensor"),
        P("section", None, "tensor"),
        P("section", None, "tensor"),
        P("section", "tensor", None),
        P("section", "tensor", None),
        P("section", None, None, "tensor"),
    )
    out_specs = P("dp", None, None, ("section", "tensor"))
    return jax.shard_map(shards, mesh=mesh, in_specs=in_specs, out_specs=out_specs, check_vma=False)
```

profile of v0, /device:TPU:0, one launch (start us, length us, event | category | flops | bytes accessed | tf_op | source)
XLA Modules:
  0.0 737.4 jit_solution(598932090509238109)
XLA Ops:
  9.2 58.9 %all-gather.3.cloned.1.call-done = bf16[4,2,64,2560]{2,0,1,3:T(4,128)(2,1)} async-done(((bf16[4,2,64,160]{2,0,1,3:T(4,128)(2,1)}), bf16[4,2,64,2560]{2,0,1,3:T(4,128)(2,1)}) %all-gather.3.cloned.1.call-update) | async-done | bytes 2621456 | tf_op jit(solution)/shard_map/all_gather | solution.py:126
  68.1 8.5 %copy.28 = bf16[4,2,64,2560]{3,2,1,0:T(8,128)(2,1)} copy(bf16[4,2,64,2560]{2,0,1,3:T(4,128)(2,1)} %all-gather.3.cloned.1.call-done) | data formatting | bytes 5242880 | tf_op jit(solution)/shard_map/while | solution.py:207
  77.5 579.8 %while.17 = (s32[]{:T(128)}, bf16[128,640]{1,0:T(8,128)(2,1)S(1)}, bf16[4,128,640]{2,1,0:T(8,128)(2,1)}, pred[]{:T(512)}, s32[4]{0:T(128)S(1)}, /*index=5*/bf16[...) while((s32[]{:T(128)}, bf16[128,640]{1,0:T(8,128)(2,1)S(1)}, ...), condition=%wide.region_10.11_spmd, body=%wide.region_0.10_spmd.sunk | while | flops 1744747648 | bytes 44909328 | solution.py:207
  82.6 7.9 %all_gather.19 = bf16[128,2560]{1,0:T(8,128)(2,1)S(1)} all-gather(bf16[128,640]{1,0:T(8,128)(2,1)S(1)} %dynamic-slice_select_fusion.2), channel_id=1, replica_groups=mesh['section'=4,'dp'=2,'tensor'=4] {'tensor'}, dimensions={1}, use_global_device_ids=true | all-gather | bytes 819200 | tf_op jit(solution)/shard_map/while/body/eval_jaxpr/all_gather | solution.py:196
  90.5 2.5 conditional.4
  93.0 11.1 %psum.23 = bf16[128,128]{1,0:T(8,128)(2,1)S(1)} all-reduce(f32[128,128]{1,0:T(8,128)S(1)} %get-tuple-element.638), channel_id=1, replica_groups=mesh['section'=4,'dp'=2,'tensor'=4] {'tensor'}, use_global_device_ids=true, to_apply=%region_4.4 | all-reduce | flops 16384 | bytes 98304 | tf_op jit(solution)/shard_map/while/body/eval_jaxpr/psum | solution.py:153
  105.1 22.0 %conditional.5 = (bf16[128,2560]{1,0:T(8,128)(2,1)S(1)}) conditional(s32[]{:T(128)} %convert_element_type.120, () %tuple.63, (bf16[1,2560,640]{2,1,0:T(8,128)(2,1)}, bf16[128,2560]{1,0:T(8,128)(2,1)}, bf16[128,128]{1,0:T(8,128)(2,1)S(1)}, bf16[1,2,64,640]{3,2,1,0:T(8,128)(2,1)}, bf16[1,2560,640]{2,1,0:T(8,128)(2,1)}, ...), branch_computations={%region_5.5_spmd, %region_6.8_spmd} | conditional | flops 1720939136 | bytes 34157632 | solution.py:160
  106.2 3.5 fusion.18
  111.7 3.5 fusion.24
  119.5 2.4 fusion.21
  124.5 2.6 fusion.1
  128.3 20.7 %reduce-scatter.6.cloned.1.call-done = bf16[640,128]{1,0:T(8,128)(2,1)} async-done(((bf16[2560,128]{1,0:T(8,128)(2,1)}), bf16[640,128]{1,0:T(8,128)(2,1)}) %reduce-scatter.6.cloned.1.call-update) | async-done | bytes 163856 | tf_op jit(solution)/shard_map/while
  151.7 3.4 collective-permute-start
  155.1 3.2 collective-permute-done
  163.4 7.0 all_gather.19
  170.3 2.5 conditional.4
  172.9 12.0 %psum.23 = bf16[128,128]{1,0:T(8,128)(2,1)S(1)} all-reduce(f32[128,128]{1,0:T(8,128)S(1)} %get-tuple-element.638), channel_id=1, replica_groups=mesh['section'=4,'dp'=2,'tensor'=4] {'tensor'}, use_global_device_ids=true, to_apply=%region_4.4 | all-reduce | flops 16384 | bytes 98304 | tf_op jit(solution)/shard_map/while/body/eval_jaxpr/psum | solution.py:153
  185.8 22.1 %conditional.5 = (bf16[128,2560]{1,0:T(8,128)(2,1)S(1)}) conditional(s32[]{:T(128)} %convert_element_type.120, () %tuple.63, (bf16[1,2560,640]{2,1,0:T(8,128)(2,1)}, bf16[128,2560]{1,0:T(8,128)(2,1)}, bf16[128,128]{1,0:T(8,128)(2,1)S(1)}, bf16[1,2,64,640]{3,2,1,0:T(8,128)(2,1)}, bf16[1,2560,640]{2,1,0:T(8,128)(2,1)}, ...), branch_computations={%region_5.5_spmd, %region_6.8_spmd} | conditional | flops 1720939136 | bytes 34157632 | solution.py:160
  186.9 3.5 fusion.18
  192.3 3.5 fusion.24
  200.2 2.4 fusion.21
  205.2 2.6 fusion.1
  209.0 21.8 %reduce-scatter.6.cloned.1.call-done = bf16[640,128]{1,0:T(8,128)(2,1)} async-done(((bf16[2560,128]{1,0:T(8,128)(2,1)}), bf16[640,128]{1,0:T(8,128)(2,1)}) %reduce-scatter.6.cloned.1.call-update) | async-done | bytes 163856 | tf_op jit(solution)/shard_map/while
  233.5 3.4 collective-permute-start
  236.9 3.3 collective-permute-done
  245.2 7.0 all_gather.19
  252.1 2.5 conditional.4
  254.7 12.0 %psum.23 = bf16[128,128]{1,0:T(8,128)(2,1)S(1)} all-reduce(f32[128,128]{1,0:T(8,128)S(1)} %get-tuple-element.638), channel_id=1, replica_groups=mesh['section'=4,'dp'=2,'tensor'=4] {'tensor'}, use_global_device_ids=true, to_apply=%region_4.4 | all-reduce | flops 16384 | bytes 98304 | tf_op jit(solution)/shard_map/while/body/eval_jaxpr/psum | solution.py:153
  267.6 22.1 %conditional.5 = (bf16[128,2560]{1,0:T(8,128)(2,1)S(1)}) conditional(s32[]{:T(128)} %convert_element_type.120, () %tuple.63, (bf16[1,2560,640]{2,1,0:T(8,128)(2,1)}, bf16[128,2560]{1,0:T(8,128)(2,1)}, bf16[128,128]{1,0:T(8,128)(2,1)S(1)}, bf16[1,2,64,640]{3,2,1,0:T(8,128)(2,1)}, bf16[1,2560,640]{2,1,0:T(8,128)(2,1)}, ...), branch_computations={%region_5.5_spmd, %region_6.8_spmd} | conditional | flops 1720939136 | bytes 34157632 | solution.py:160
  268.7 3.5 fusion.18
  274.2 3.5 fusion.24
  282.0 2.4 fusion.21
  287.0 2.6 fusion.1
  290.8 22.7 %reduce-scatter.6.cloned.1.call-done = bf16[640,128]{1,0:T(8,128)(2,1)} async-done(((bf16[2560,128]{1,0:T(8,128)(2,1)}), bf16[640,128]{1,0:T(8,128)(2,1)}) %reduce-scatter.6.cloned.1.call-update) | async-done | bytes 163856 | tf_op jit(solution)/shard_map/while
  316.2 3.4 collective-permute-start
  319.6 3.2 collective-permute-done
  327.9 7.0 all_gather.19
  334.8 2.5 conditional.4
  337.4 12.0 %psum.23 = bf16[128,128]{1,0:T(8,128)(2,1)S(1)} all-reduce(f32[128,128]{1,0:T(8,128)S(1)} %get-tuple-element.638), channel_id=1, replica_groups=mesh['section'=4,'dp'=2,'tensor'=4] {'tensor'}, use_global_device_ids=true, to_apply=%region_4.4 | all-reduce | flops 16384 | bytes 98304 | tf_op jit(solution)/shard_map/while/body/eval_jaxpr/psum | solution.py:153
  350.3 22.1 %conditional.5 = (bf16[128,2560]{1,0:T(8,128)(2,1)S(1)}) conditional(s32[]{:T(128)} %convert_element_type.120, () %tuple.63, (bf16[1,2560,640]{2,1,0:T(8,128)(2,1)}, bf16[128,2560]{1,0:T(8,128)(2,1)}, bf16[128,128]{1,0:T(8,128)(2,1)S(1)}, bf16[1,2,64,640]{3,2,1,0:T(8,128)(2,1)}, bf16[1,2560,640]{2,1,0:T(8,128)(2,1)}, ...), branch_computations={%region_5.5_spmd, %region_6.8_spmd} | conditional | flops 1720939136 | bytes 34157632 | solution.py:160
  351.4 3.5 fusion.18
  356.9 3.5 fusion.24
  364.7 2.4 fusion.21
  369.7 2.6 fusion.1
  373.5 23.6 %reduce-scatter.6.cloned.1.call-done = bf16[640,128]{1,0:T(8,128)(2,1)} async-done(((bf16[2560,128]{1,0:T(8,128)(2,1)}), bf16[640,128]{1,0:T(8,128)(2,1)}) %reduce-scatter.6.cloned.1.call-update) | async-done | bytes 163856 | tf_op jit(solution)/shard_map/while
  399.8 3.4 collective-permute-start
  403.2 3.3 collective-permute-done
  411.5 7.0 all_gather.19
  419.3 12.0 %psum.23 = bf16[128,128]{1,0:T(8,128)(2,1)S(1)} all-reduce(f32[128,128]{1,0:T(8,128)S(1)} %get-tuple-element.638), channel_id=1, replica_groups=mesh['section'=4,'dp'=2,'tensor'=4] {'tensor'}, use_global_device_ids=true, to_apply=%region_4.4 | all-reduce | flops 16384 | bytes 98304 | tf_op jit(solution)/shard_map/while/body/eval_jaxpr/psum | solution.py:153
  433.5 47.2 %reduce-scatter.6.cloned.1.call-done = bf16[640,128]{1,0:T(8,128)(2,1)} async-done(((bf16[2560,128]{1,0:T(8,128)(2,1)}), bf16[640,128]{1,0:T(8,128)(2,1)}) %reduce-scatter.6.cloned.1.call-update) | async-done | bytes 163856 | tf_op jit(solution)/shard_map/while
  483.4 3.4 collective-permute-start
  486.8 3.3 collective-permute-done
  495.1 6.9 all_gather.19
  502.9 12.0 %psum.23 = bf16[128,128]{1,0:T(8,128)(2,1)S(1)} all-reduce(f32[128,128]{1,0:T(8,128)S(1)} %get-tuple-element.638), channel_id=1, replica_groups=mesh['section'=4,'dp'=2,'tensor'=4] {'tensor'}, use_global_device_ids=true, to_apply=%region_4.4 | all-reduce | flops 16384 | bytes 98304 | tf_op jit(solution)/shard_map/while/body/eval_jaxpr/psum | solution.py:153
  517.1 47.2 %reduce-scatter.6.cloned.1.call-done = bf16[640,128]{1,0:T(8,128)(2,1)} async-done(((bf16[2560,128]{1,0:T(8,128)(2,1)}), bf16[640,128]{1,0:T(8,128)(2,1)}) %reduce-scatter.6.cloned.1.call-update) | async-done | bytes 163856 | tf_op jit(solution)/shard_map/while
  567.0 3.4 collective-permute-start
  570.4 3.3 collective-permute-done
  578.7 6.9 all_gather.19
  586.5 12.0 %psum.23 = bf16[128,128]{1,0:T(8,128)(2,1)S(1)} all-reduce(f32[128,128]{1,0:T(8,128)S(1)} %get-tuple-element.638), channel_id=1, replica_groups=mesh['section'=4,'dp'=2,'tensor'=4] {'tensor'}, use_global_device_ids=true, to_apply=%region_4.4 | all-reduce | flops 16384 | bytes 98304 | tf_op jit(solution)/shard_map/while/body/eval_jaxpr/psum | solution.py:153
  600.7 47.2 %reduce-scatter.6.cloned.1.call-done = bf16[640,128]{1,0:T(8,128)(2,1)} async-done(((bf16[2560,128]{1,0:T(8,128)(2,1)}), bf16[640,128]{1,0:T(8,128)(2,1)}) %reduce-scatter.6.cloned.1.call-update) | async-done | bytes 163856 | tf_op jit(solution)/shard_map/while
  650.6 3.4 collective-permute-start
  654.0 3.3 collective-permute-done
  658.3 43.7 %all-reduce.2.cloned.1.call-done = bf16[4,128,640]{2,1,0:T(8,128)(2,1)} async-done(((bf16[4,128,640]{2,1,0:T(8,128)(2,1)}), bf16[4,128,640]{2,1,0:T(8,128)(2,1)}) %all-reduce.2.cloned.1.call-update) | async-done | bytes 655376 | tf_op jit(solution)/shard_map/psum | solution.py:22
  702.0 26.7 %all-gather.5.cloned.1.call-done = bf16[4,128,2560]{2,1,0:T(8,128)(2,1)} async-done(((bf16[4,128,640]{2,1,0:T(8,128)(2,1)}), bf16[4,128,2560]{2,1,0:T(8,128)(2,1)}) %all-gather.5.cloned.1.call-update) | async-done | bytes 2621456 | tf_op jit(solution)/shard_map/all_gather | solution.py:209
  (198 shorter events, 103.5 us)
Async XLA Ops:
  6.5 61.6 %all-gather.3.cloned.1.call-start = ((), (), s32[]{:S(2)}) async-start(), calls=%async_computation.1 | async-start | bytes 5570560 | tf_op jit(solution)/shard_map/all_gather | solution.py:126
  9.2 68.3 %copy-start.1 = (f32[1,2560]{1,0:T(1,128)S(1)}, f32[1,2560]{1,0:T(1,128)}, u32[]{:S(2)}) copy-start(f32[1,2560]{1,0:T(1,128)} %param.19) | copy-start | bytes 30724
  9.2 68.3 %copy-start.2 = (s32[4]{0:T(128)S(1)}, s32[4]{0:T(128)}, u32[]{:S(2)}) copy-start(s32[4]{0:T(128)} %param.18) | copy-start | bytes 52
  77.5 71.5 %reduce-scatter.6.cloned.1.call-start = ((), (), s32[]{:S(2)}) async-start(), calls=%async_computation.4 | async-start | bytes 819200 | tf_op jit(solution)/shard_map/while
  109.7 9.8 %copy-start = (bf16[1,2560,640]{2,1,0:T(8,128)(2,1)S(1)}, bf16[1,2560,640]{2,1,0:T(8,128)(2,1)}, u32[]{:S(2)}) copy-start(bf16[1,2560,640]{2,1,0:T(8,128)(2,1)} %get-tuple-element.398) | copy-start | bytes 9830404 | tf_op jit(solution)/shard_map/while/body/eval_jaxpr/cond
  118.2 1.3 copy-start.3
  151.7 6.6 collective-permute-start
  158.3 72.4 %reduce-scatter.6.cloned.1.call-start = ((), (), s32[]{:S(2)}) async-start(), calls=%async_computation.4 | async-start | bytes 819200 | tf_op jit(solution)/shard_map/while
  190.3 9.8 %copy-start = (bf16[1,2560,640]{2,1,0:T(8,128)(2,1)S(1)}, bf16[1,2560,640]{2,1,0:T(8,128)(2,1)}, u32[]{:S(2)}) copy-start(bf16[1,2560,640]{2,1,0:T(8,128)(2,1)} %get-tuple-element.398) | copy-start | bytes 9830404 | tf_op jit(solution)/shard_map/while/body/eval_jaxpr/cond
  198.9 1.3 copy-start.3
  233.5 6.7 collective-permute-start
  240.2 73.3 %reduce-scatter.6.cloned.1.call-start = ((), (), s32[]{:S(2)}) async-start(), calls=%async_computation.4 | async-start | bytes 819200 | tf_op jit(solution)/shard_map/while
  272.2 9.8 %copy-start = (bf16[1,2560,640]{2,1,0:T(8,128)(2,1)S(1)}, bf16[1,2560,640]{2,1,0:T(8,128)(2,1)}, u32[]{:S(2)}) copy-start(bf16[1,2560,640]{2,1,0:T(8,128)(2,1)} %get-tuple-element.398) | copy-start | bytes 9830404 | tf_op jit(solution)/shard_map/while/body/eval_jaxpr/cond
  280.7 1.3 copy-start.3
  316.2 6.6 collective-permute-start
  322.9 74.2 %reduce-scatter.6.cloned.1.call-start = ((), (), s32[]{:S(2)}) async-start(), calls=%async_computation.4 | async-start | bytes 819200 | tf_op jit(solution)/shard_map/while
  354.9 9.8 %copy-start = (bf16[1,2560,640]{2,1,0:T(8,128)(2,1)S(1)}, bf16[1,2560,640]{2,1,0:T(8,128)(2,1)}, u32[]{:S(2)}) copy-start(bf16[1,2560,640]{2,1,0:T(8,128)(2,1)} %get-tuple-element.398) | copy-start | bytes 9830404 | tf_op jit(solution)/shard_map/while/body/eval_jaxpr/cond
  363.4 1.3 copy-start.3
  399.8 6.7 collective-permute-start
  406.4 74.2 %reduce-scatter.6.cloned.1.call-start = ((), (), s32[]{:S(2)}) async-start(), calls=%async_computation.4 | async-start | bytes 819200 | tf_op jit(solution)/shard_map/while
  483.4 6.7 collective-permute-start
  490.1 74.2 %reduce-scatter.6.cloned.1.call-start = ((), (), s32[]{:S(2)}) async-start(), calls=%async_computation.4 | async-start | bytes 819200 | tf_op jit(solution)/shard_map/while
  567.0 6.6 collective-permute-start
  573.7 74.2 %reduce-scatter.6.cloned.1.call-start = ((), (), s32[]{:S(2)}) async-start(), calls=%async_computation.4 | async-start | bytes 819200 | tf_op jit(solution)/shard_map/while
  650.6 6.7 collective-permute-start
  657.3 44.7 %all-reduce.2.cloned.1.call-start = ((), (), s32[]{:S(2)}) async-start(), calls=%async_computation.2 | async-start | bytes 1310720 | tf_op jit(solution)/shard_map/psum | solution.py:22
  658.2 70.5 %all-gather.5.cloned.1.call-start = ((), (), s32[]{:S(2)}) async-start(), calls=%async_computation.3 | async-start | bytes 3276800 | tf_op jit(solution)/shard_map/all_gather | solution.py:209
Sparse Core Ops, SparseCore 0:
  9.6 58.4 all-gather.2
  128.4 20.5 reduce-scatter.5
  209.1 21.6 reduce-scatter.5
  290.9 22.5 reduce-scatter.5
  373.6 23.4 reduce-scatter.5
  433.6 47.0 reduce-scatter.5
  517.2 47.0 reduce-scatter.5
  600.8 47.0 reduce-scatter.5
  660.4 41.5 all-reduce.1
  703.4 25.2 all-gather.4
where the time goes:
time: 740 us; the launch traced here: 737 us
  waiting for transfers between devices  383 us (52%)
  blocking collectives  133 us (18%)
  matrix products  72 us (10%)
  local copies, waits for them, and re-layouts  65.6 us (9%)
  loops' own time  27.8 us (4%)
  starting transfers between devices  23.8 us (3%)
  other arithmetic  19.2 us (3%)
  between operations  13.5 us (2%)
    while x14, waiting for transfers between devices  231 us
    psum x7, blocking collectives, compute(): summed_codes = lax.psum(part_codes, 'tensor')  83.2 us
    all_gather x1, waiting for transfers between devices, shards(): entire = lax.all_gather(inputs, ('section', 'tensor'), axis=3, tiled=True)  58.9 us
    all_gather x7, blocking collectives, advance(): complete_result = lax.all_gather(owned, 'tensor', axis=1, tiled=True)  49.7 us
    psum x1, waiting for transfers between devices, spread(): return lax.psum(jnp.where(mine, array, jnp.zeros_like(array)), axis)  43.7 us
    another operation x1, loops' own time, shards(): arrived, stored = lax.fori_loop(0, step_count, advance, (initial, stored))  27.4 us
    all_gather x1, waiting for transfers between devices, shards(): complete = lax.all_gather(result, 'tensor', axis=2, tiled=True)  26.7 us
    ppermute x7, starting transfers between devices, shifted(): lax.ppermute(value, axis, [(source, source + steps) for source in range(l...  23.7 us
  transfers between devices with their start and end apart: 17, of which 17 were waited for; matrix products, arithmetic and copies ran while one was open for 0% of the time, Pallas kernels for 0%

commit v1 on v0

v1 whole, which is shorter than its diff:
```python
import functools

import jax
import jax.numpy as jnp
from jax import lax
from jax.experimental import pallas as pl
from jax.experimental.pallas import tpu as pltpu
from jax.sharding import PartitionSpec as P

HEAD_DIM = 128
ADAPTER_RANK = 16
ADAPTER_JOBS = 4
ADAPTER_SCALE = 2.0
SEQS_PER_CHUNK = 1

F32 = jnp.float32
BF16 = jnp.bfloat16


def remote(src, dst, send, recv, section, tensor):
    return pltpu.make_async_remote_copy(
        src_ref=src,
        dst_ref=dst,
        send_sem=send,
        recv_sem=recv,
        device_id={"section": section, "tensor": tensor},
        device_id_type=pl.DeviceIdType.MESH,
    )


def kernel(
    S, T, C, CPB, CR, SEQ, F, COL, W, LR,
    entry, jobs, x_ref, gain_ref, wq, wk, wv, wo, d_ref, up_ref,
    out_ref,
    wbuf, obuf, xsel, xin, xh, xn, qkv, heads, pown, psend, precv, xs, zbuf, ostage, orecv,
    w_sem, d_send, d_recv, in_send, in_recv, px_send, px_recv, pp_send, pp_recv,
    f_send, f_recv, r_send, r_recv, x_send, x_recv, z_send, z_recv, o_send, o_recv,
):
    X = T // 2
    H = F // 2
    sec = lax.axis_index("section")
    t = lax.axis_index("tensor")
    c = lax.rem(t, 2)
    x = t // 2
    partner = t + 1 - 2 * c
    nseq = CR // SEQ
    heads_n = COL // HEAD_DIM

    loads = [
        pltpu.make_async_copy(wq.at[0], wbuf.at[:, pl.ds(0, COL)], w_sem.at[0]),
        pltpu.make_async_copy(wk.at[0], wbuf.at[:, pl.ds(COL, COL)], w_sem.at[1]),
        pltpu.make_async_copy(wv.at[0], wbuf.at[:, pl.ds(2 * COL, COL)], w_sem.at[2]),
        pltpu.make_async_copy(wo.at[0, :, pl.ds(0, H)], obuf.at[0], w_sem.at[3]),
        pltpu.make_async_copy(wo.at[0, :, pl.ds(H, H)], obuf.at[1], w_sem.at[4]),
    ]

    for p in range(C):
        xsel[p] = x_ref[entry[p // CPB], (p % CPB) * CR : (p % CPB + 1) * CR, :]

    barrier = pltpu.get_barrier_semaphore()
    me = sec * T + t
    for step in range(1, S * T):
        other = lax.rem(me + step, S * T)
        pl.semaphore_signal(
            barrier,
            inc=1,
            device_id={"section": other // T, "tensor": lax.rem(other, T)},
            device_id_type=pl.DeviceIdType.MESH,
        )
    for load in loads:
        load.start()
    pl.semaphore_wait(barrier, S * T - 1)

    def in_copy(p, from_sec):
        return remote(
            xsel.at[p], xin.at[p, t, from_sec], in_send.at[p], in_recv.at[p, from_sec], 0, t
        )

    @pl.when(sec > 0)
    def _():
        for p in range(C):
            in_copy(p, sec).start()

    @pl.when(sec == 0)
    def _():
        for p in range(C):
            xin[p, t, 0] = xsel[p]

    def d_rows(owner):
        return wbuf.at[pl.ds(pl.multiple_of(owner * COL, COL), COL), pl.ds(3 * COL, LR)]

    def d_peer(k):
        return remote(
            d_ref.at[0], d_rows(t), d_send.at[k], d_recv.at[k], sec, lax.rem(x + k, X) * 2 + c
        )

    def d_own():
        return remote(d_ref.at[0], d_rows(t), d_send.at[0], d_recv.at[0], sec, partner)

    def d_forward(k):
        owner = lax.rem(x - k + X, X) * 2 + c
        return remote(
            d_rows(owner), d_rows(owner), d_send.at[X + k], d_recv.at[X + k], sec, partner
        )

    for k in range(1, X):
        d_peer(k).start()
    d_own().start()
    wbuf[pl.ds(pl.multiple_of(t * COL, COL), COL), 3 * COL :] = d_ref[0]

    def px_copy(p, k):
        return remote(
            xin.at[p, t], xin.at[p, t], px_send.at[p, k], px_recv.at[p, k],
            sec, lax.rem(x + k, X) * 2 + c,
        )

    def pp_copy(p, k):
        owner = lax.rem(x - k + X, X) * 2 + c
        return remote(
            xin.at[p, owner], xin.at[p, owner], pp_send.at[p, k], pp_recv.at[p, k], sec, partner
        )

    def gather_a(p):
        for s in range(1, S):
            in_copy(p, s).wait_recv()
        for k in range(1, X):
            px_copy(p, k).start()
        pp_copy(p, 0).start()

    def gather_b(p):
        for k in range(1, X):
            px_copy(p, k).wait_recv()
            pp_copy(p, k).start()

    def gather_c(p):
        for k in range(X):
            pp_copy(p, k).wait_recv()
        half = S * T // 2
        for piece in range(S * T):
            column = (piece % half) * W
            xh[p, piece // half, :, column : column + W] = xin[p, piece % T, piece // T]

    def forward(p):
        return remote(xh.at[p, c], xh.at[p, c], f_send.at[p], f_recv.at[p], sec, partner)

    def z_copy(p):
        return remote(zbuf.at[p], xh.at[p, c], z_send.at[p], z_recv.at[p], sec + 1, t)

    def r_copy(p):
        return remote(psend.at[p], precv.at[p], r_send.at[p], r_recv.at[p], sec, partner)

    def x_copy(p, k):
        return remote(
            xs.at[p, x], xs.at[p, x], x_send.at[p, k], x_recv.at[p, k],
            sec, lax.rem(x + k, X) * 2 + c,
        )

    def o_copy(p, js, cc):
        return remote(
            ostage.at[p, js * 2 + cc], orecv.at[p], o_send.at[p, js * 2 + cc], o_recv.at[p],
            c * (S // 2) + js, 2 * x + cc,
        )

    causal = lax.broadcasted_iota(jnp.int32, (SEQ, SEQ), 0) >= lax.broadcasted_iota(
        jnp.int32, (SEQ, SEQ), 1
    )
    column_job = lax.broadcasted_iota(jnp.int32, (SEQ, LR), 1) // ADAPTER_RANK % ADAPTER_JOBS

    def front(p):
        halves = [xh[p, h].astype(F32) for h in range(2)]
        ssq = sum(jnp.sum(v * v, axis=-1, keepdims=True) for v in halves)
        scale = lax.rsqrt(ssq * (1.0 / F) + 1e-5)
        for h in range(2):
            xn[:, h * H : (h + 1) * H] = (
                xh[p, h].astype(F32) * scale * gain_ref[:, h * H : (h + 1) * H]
            ).astype(BF16)
        width = wbuf.shape[1]
        block = 512 if width % 512 == 0 else width
        for n in range(0, width, block):
            qkv[:, n : n + block] = jnp.dot(
                xn[...], wbuf[:, n : n + block], preferred_element_type=F32
            )
        for q in range(nseq):
            rows = slice(q * SEQ, (q + 1) * SEQ)
            index = p * nseq + q
            job = jobs[entry[p // CPB], lax.rem(index, CPB * nseq)]
            codes = jnp.where(column_job == job, qkv[rows, 3 * COL :], 0.0).astype(BF16)
            mid = LR // 2
            query = (
                qkv[rows, 0:COL]
                + ADAPTER_SCALE
                * jnp.dot(codes[:, :mid], up_ref[0, 0], preferred_element_type=F32)
            ).astype(BF16)
            keys = qkv[rows, COL : 2 * COL].astype(BF16)
            values = (
                qkv[rows, 2 * COL : 3 * COL]
                + ADAPTER_SCALE
                * jnp.dot(codes[:, mid:], up_ref[0, 1], preferred_element_type=F32)
            ).astype(BF16)
            for h in range(heads_n):
                cols = slice(h * HEAD_DIM, (h + 1) * HEAD_DIM)
                scores = (
                    lax.dot_general(
                        query[:, cols], keys[:, cols], (((1,), (1,)), ((), ())),
                        preferred_element_type=F32,
                    )
                    * HEAD_DIM**-0.5
                )
                scores = jnp.where(causal, scores, -jnp.inf)
                weights = jnp.exp(scores - jnp.max(scores, axis=-1, keepdims=True))
                probs = (weights / jnp.sum(weights, axis=-1, keepdims=True)).astype(BF16)
                heads[rows, cols] = jnp.dot(
                    probs, values[:, cols], preferred_element_type=F32
                ).astype(BF16)
        psend[p] = jnp.dot(heads[...], obuf[1 - c], preferred_element_type=F32).astype(BF16)
        r_copy(p).start()
        pown[...] = jnp.dot(heads[...], obuf[c], preferred_element_type=F32)

    def reduce_pair(p):
        r_copy(p).wait_recv()
        xs[p, x] = (pown[...] + precv[p].astype(F32)).astype(BF16)
        for k in range(1, X):
            x_copy(p, k).start()

    def finish(p):
        for k in range(1, X):
            x_copy(p, k).wait_recv()
        total = xs[p, 0].astype(F32)
        for k in range(1, X):
            total = total + xs[p, k].astype(F32)
        zbuf[p] = (xh[p, c].astype(F32) + total).astype(BF16)

        @pl.when(sec < S - 1)
        def _():
            z_copy(p).start()

        @pl.when(sec == S - 1)
        def _():
            for js in range(S // 2):
                for cc in range(2):
                    for xx in range(X):
                        column = (js * T + 2 * xx + cc) * W

                        @pl.when(x == xx)
                        def _():
                            ostage[p, js * 2 + cc] = zbuf[p, :, column : column + W]

                    mine = jnp.logical_and(c * (S // 2) + js == sec, 2 * x + cc == t)

                    @pl.when(mine)
                    def _():
                        orecv[p] = ostage[p, js * 2 + cc]

                    @pl.when(jnp.logical_not(mine))
                    def _():
                        o_copy(p, js, cc).start()

    @pl.when(sec == 0)
    def _():
        gather_a(0)
        gather_b(0)

    for k in range(1, X):
        d_peer(k).wait_recv()
        d_forward(k).start()
    d_own().wait_recv()
    for k in range(1, X):
        d_forward(k).wait_recv()
    for load in loads:
        load.wait()

    def body(p, carry):
        @pl.when(sec == 0)
        def _():
            @pl.when(p + 1 < C)
            def _():
                gather_a(p + 1)

            gather_c(p)

        @pl.when(sec > 0)
        def _():
            z_copy(p).wait_recv()
            forward(p).start()

        @pl.when(p > 0)
        def _():
            reduce_pair(p - 1)

        @pl.when(sec > 0)
        def _():
            forward(p).wait_recv()

        front(p)

        @pl.when(jnp.logical_and(sec == 0, p + 1 < C))
        def _():
            gather_b(p + 1)

        @pl.when(p > 0)
        def _():
            finish(p - 1)

        return carry

    lax.fori_loop(0, C, body, 0)
    reduce_pair(C - 1)
    finish(C - 1)

    is_local = jnp.logical_and(sec == S - 1, c == 1)

    def drain(p, carry):
        @pl.when(jnp.logical_not(is_local))
        def _():
            o_copy(p, 0, 0).wait_recv()

        out_ref[p] = orecv[p]
        r_copy(p).wait_send()
        for k in range(1, X):
            x_copy(p, k).wait_send()

        @pl.when(sec > 0)
        def _():
            in_copy(p, sec).wait_send()
            forward(p).wait_send()

        @pl.when(sec == 0)
        def _():
            pp_copy(p, 0).wait_send()
            for k in range(1, X):
                px_copy(p, k).wait_send()
                pp_copy(p, k).wait_send()

        @pl.when(sec < S - 1)
        def _():
            z_copy(p).wait_send()

        @pl.when(sec == S - 1)
        def _():
            for js in range(S // 2):
                for cc in range(2):
                    mine = jnp.logical_and(c * (S // 2) + js == sec, 2 * x + cc == t)

                    @pl.when(jnp.logical_not(mine))
                    def _():
                        o_copy(p, js, cc).wait_send()

        return carry

    lax.fori_loop(0, C, drain, 0)
    d_own().wait_send()
    for k in range(1, X):
        d_peer(k).wait_send()
        d_forward(k).wait_send()


def solution(mesh):
    S, T = mesh.shape["section"], mesh.shape["tensor"]

    def shards(inputs, sequence_jobs, entry_sequence, gain, wq, wk, wv, wo, down, up):
        batches, nseq, seq, W = inputs.shape
        F, COL = wq.shape[1], wq.shape[2]
        LR = down.shape[2]
        CR = SEQS_PER_CHUNK * seq
        CPB = nseq // SEQS_PER_CHUNK
        C = batches * CPB
        X, H = T // 2, F // 2
        vmem = pl.BlockSpec(memory_space=pltpu.VMEM)
        smem = pl.BlockSpec(memory_space=pltpu.SMEM)
        anym = pl.BlockSpec(memory_space=pl.ANY)
        dma = pltpu.SemaphoreType.DMA
        out = pl.pallas_call(
            functools.partial(kernel, S, T, C, CPB, CR, seq, F, COL, W, LR),
            out_shape=jax.ShapeDtypeStruct((C, CR, W), BF16),
            in_specs=[smem, smem, vmem, vmem, anym, anym, anym, anym, vmem, vmem],
            out_specs=vmem,
            scratch_shapes=[
                pltpu.VMEM((F, 3 * COL + LR), BF16),
                pltpu.VMEM((2, COL, H), BF16),
                pltpu.VMEM((C, CR, W), BF16),
                pltpu.VMEM((C, T, S, CR, W), BF16),
                pltpu.VMEM((C, 2, CR, H), BF16),
                pltpu.VMEM((CR, F), BF16),
                pltpu.VMEM((CR, 3 * COL + LR), F32),
                pltpu.VMEM((CR, COL), BF16),
                pltpu.VMEM((CR, H), F32),
                pltpu.VMEM((C, CR, H), BF16),
                pltpu.VMEM((C, CR, H), BF16),
                pltpu.VMEM((C, X, CR, H), BF16),
                pltpu.VMEM((C, CR, H), BF16),
                pltpu.VMEM((C, S, CR, W), BF16),
                pltpu.VMEM((C, CR, W), BF16),
                dma((5,)),
                dma((2 * X,)), dma((2 * X,)),
                dma((C,)), dma((C, S)),
                dma((C, X)), dma((C, X)),
                dma((C, X)), dma((C, X)),
                dma((C,)), dma((C,)),
                dma((C,)), dma((C,)),
                dma((C, X)), dma((C, X)),
                dma((C,)), dma((C,)),
                dma((C, S)), dma((C,)),
            ],
            compiler_params=pltpu.CompilerParams(
                collective_id=0, has_side_effects=True, vmem_limit_bytes=60 * 1024 * 1024
            ),
        )(
            entry_sequence, sequence_jobs[:, :, 0], inputs.reshape(batches, nseq * seq, W),
            gain, wq, wk, wv, wo, down, up,
        )
        return out.reshape(batches, nseq, seq, W)

    return jax.shard_map(
        shards,
        mesh=mesh,
        in_specs=(
            P("dp", None, None, ("section", "tensor")),
            P("dp", None, None),
            P("dp"),
            P("section", None),
            P("section", None, "tensor"),
            P("section", None, "tensor"),
            P("section", None, "tensor"),
            P("section", "tensor", None),
            P("section", "tensor", None),
            P("section", None, None, "tensor"),
        ),
        out_specs=P("dp", None, None, ("section", "tensor")),
        check_vma=False,
    )
```

time: 740 us -> 147 us (0.20)
  waiting for transfers between devices: 383 us -> 0 us
  Pallas kernels: 0 us -> 144 us
  blocking collectives: 133 us -> 0 us
  matrix products: 72 us -> 0 us
  local copies, waits for them, and re-layouts: 65.6 us -> 3.01 us
  loops' own time: 27.8 us -> 0 us
  starting transfers between devices: 23.8 us -> 0 us
  other arithmetic: 19.2 us -> 0 us
  between operations: 13.5 us -> 0.01 us
    while x14 -> x0, waiting for transfers between devices: 231 us -> none
    pallas_call x0 -> x1, Pallas kernels: none -> 144 us  [shards(): pl.pallas_call(functools.partial(kernel, S, T, C, CPB, CR, seq, F, COL, W...]
    all_gather x2 -> x0, waiting for transfers between devices: 85.5 us -> none  [the longest x1 58.9 us: shards(): entire = lax.all_gather(inputs, ('section', 'tensor'), axis=3, tiled=True)]
    psum x7 -> x0, blocking collectives: 83.2 us -> none  [compute(): summed_codes = lax.psum(part_codes, 'tensor')]
    dot_general x36 -> x0, matrix products: 72 us -> none  [the longest x4 14 us: final_output(): jnp.dot(normalized_input, query_matrix, preferred_element_type=jnp.float32)]
    all_gather x7 -> x0, blocking collectives: 49.7 us -> none  [advance(): complete_result = lax.all_gather(owned, 'tensor', axis=1, tiled=True)]
    psum x1 -> x0, waiting for transfers between devices: 43.7 us -> none  [spread(): return lax.psum(jnp.where(mine, array, jnp.zeros_like(array)), axis)]
    another operation x15 -> x0, loops' own time: 27.8 us -> none  [the longest x1 27.4 us: shards(): arrived, stored = lax.fori_loop(0, step_count, advance, (initial, stored))]
  transfers between devices with their start and end apart: 17 -> 0, of which waited for: 17 -> 0; matrix products, arithmetic and copies ran while one was open for 0% -> 0% of each run, Pallas kernels for 0% -> 0%
where the time goes in v1:
time: 147 us
  Pallas kernels  144 us (98%)
  local copies, waits for them, and re-layouts  3.01 us (2%)
    pallas_call x1, Pallas kernels, shards(): pl.pallas_call(functools.partial(kernel, S, T, C, CPB, CR, seq, F, COL, W...  144 us

profile of v1, /device:TPU:0, one launch (start us, length us, event | category | flops | bytes accessed | tf_op | source)
XLA Modules:
  0.0 147.1 jit_solution(9163810928826838665)
XLA Ops:
  0.0 1.3 copy.11.jobs
  1.3 144.1 %shard_map.100 = bf16[8,64,160]{2,1,0:T(8,128)(2,1)} custom-call(s32[4]{0:T(128)} %entry.1, s32[4,2]{1,0:T(4,128)} %copy.11.jobs, bf16[4,128,160]{2,1,0:T(8,128)(2,1)} %bitcast.4, f32[1,2560]{1,0:T(1,128)} %gain_ref.1, bf16[1,2560,640]{2,1,0:T(8,128)(2,1)} %wq.1, bf16[1,2560,640]{2,1,0:T(8,128)(2,1)} %wk.1, bf16[1,2560,640]{2,1,0:T(8,128)(2,1)} %wv.1, ...), custom_call_target="tpu_custom_call" | custom-call | tf_op jit(solution)/shard_map/pallas_call | solution.py:372
  145.4 1.7 %copy.13 = bf16[4,2,64,160]{3,2,1,0:T(8,128)(2,1)} copy(bf16[4,2,64,160]{3,2,1,0:T(8,128)(2,1)} %bitcast.3) | data formatting | bytes 327680

commit v2 on v1

--- a/solution.py
+++ b/solution.py
@@ -12,6 +12,8 @@
 ADAPTER_JOBS = 4
 ADAPTER_SCALE = 2.0
 SEQS_PER_CHUNK = 1
+PIECES = 2
+IN_FLIGHT = 1
 
 F32 = jnp.float32
 BF16 = jnp.bfloat16
@@ -28,12 +30,17 @@
     )
 
 
+def packing(W):
+    whole, rest = W // 128, W % 128
+    return whole, rest, 128 // rest if rest and 128 % rest == 0 else 1
+
+
 def kernel(
     S, T, C, CPB, CR, SEQ, F, COL, W, LR,
     entry, jobs, x_ref, gain_ref, wq, wk, wv, wo, d_ref, up_ref,
     out_ref,
     wbuf, obuf, xsel, xin, xh, xn, qkv, heads, pown, psend, precv, xs, zbuf, ostage, orecv,
-    w_sem, d_send, d_recv, in_send, in_recv, px_send, px_recv, pp_send, pp_recv,
+    w_sem, d_send, d_recv, in_send, in_recv, pp_send, pp_recv,
     f_send, f_recv, r_send, r_recv, x_send, x_recv, z_send, z_recv, o_send, o_recv,
 ):
     X = T // 2
@@ -54,8 +61,17 @@
         pltpu.make_async_copy(wo.at[0, :, pl.ds(H, H)], obuf.at[1], w_sem.at[4]),
     ]
 
+    whole, rest, groups = packing(W)
+    RG = CR // groups
     for p in range(C):
-        xsel[p] = x_ref[entry[p // CPB], (p % CPB) * CR : (p % CPB + 1) * CR, :]
+        value = x_ref[entry[p // CPB], (p % CPB) * CR : (p % CPB + 1) * CR, :]
+        for b in range(whole):
+            xsel[p, b * CR : (b + 1) * CR, :128] = value[:, b * 128 : (b + 1) * 128]
+        if rest:
+            for g in range(groups):
+                xsel[p, whole * CR : whole * CR + RG, g * rest : (g + 1) * rest] = value[
+                    g * RG : (g + 1) * RG, whole * 128 :
+                ]
 
     barrier = pltpu.get_barrier_semaphore()
     me = sec * T + t
@@ -71,20 +87,27 @@
         load.start()
     pl.semaphore_wait(barrier, S * T - 1)
 
-    def in_copy(p, from_sec):
-        return remote(
-            xsel.at[p], xin.at[p, t, from_sec], in_send.at[p], in_recv.at[p, from_sec], 0, t
-        )
-
-    @pl.when(sec > 0)
-    def _():
-        for p in range(C):
-            in_copy(p, sec).start()
-
-    @pl.when(sec == 0)
-    def _():
-        for p in range(C):
+    def in_copy(p, k, from_sec):
+        return remote(
+            xsel.at[p], xin.at[p, t, from_sec], in_send.at[p, k], in_recv.at[p, k, from_sec],
+            0, lax.rem(x + k, X) * 2 + c,
+        )
+
+    for p in range(C):
+
+        @pl.when(sec > 0)
+        def _():
+            if p >= IN_FLIGHT:
+                for k in range(X):
+                    in_copy(p - IN_FLIGHT, k, sec).wait_send()
+            in_copy(p, 0, sec).start()
+
+        @pl.when(sec == 0)
+        def _():
             xin[p, t, 0] = xsel[p]
+
+        for k in range(1, X):
+            in_copy(p, k, sec).start()
 
     def d_rows(owner):
         return wbuf.at[pl.ds(pl.multiple_of(owner * COL, COL), COL), pl.ds(3 * COL, LR)]
@@ -108,12 +131,6 @@
     d_own().start()
     wbuf[pl.ds(pl.multiple_of(t * COL, COL), COL), 3 * COL :] = d_ref[0]
 
-    def px_copy(p, k):
-        return remote(
-            xin.at[p, t], xin.at[p, t], px_send.at[p, k], px_recv.at[p, k],
-            sec, lax.rem(x + k, X) * 2 + c,
-        )
-
     def pp_copy(p, k):
         owner = lax.rem(x - k + X, X) * 2 + c
         return remote(
@@ -121,15 +138,9 @@
         )
 
     def gather_a(p):
-        for s in range(1, S):
-            in_copy(p, s).wait_recv()
-        for k in range(1, X):
-            px_copy(p, k).start()
-        pp_copy(p, 0).start()
-
-    def gather_b(p):
-        for k in range(1, X):
-            px_copy(p, k).wait_recv()
+        for k in range(X):
+            for s in range(1 if k == 0 else 0, S):
+                in_copy(p, k, s).wait_recv()
             pp_copy(p, k).start()
 
     def gather_c(p):
@@ -138,20 +149,40 @@
         half = S * T // 2
         for piece in range(S * T):
             column = (piece % half) * W
-            xh[p, piece // half, :, column : column + W] = xin[p, piece % T, piece // T]
-
-    def forward(p):
-        return remote(xh.at[p, c], xh.at[p, c], f_send.at[p], f_recv.at[p], sec, partner)
-
-    def z_copy(p):
-        return remote(zbuf.at[p], xh.at[p, c], z_send.at[p], z_recv.at[p], sec + 1, t)
+            side, owner, level = piece // half, piece % T, piece // T
+            for b in range(whole):
+                xh[p, side, :, column + b * 128 : column + (b + 1) * 128] = xin[
+                    p, owner, level, b * CR : (b + 1) * CR, :128
+                ]
+            if rest:
+                column += whole * 128
+                for g in range(groups):
+                    xh[p, side, g * RG : (g + 1) * RG, column : column + rest] = xin[
+                        p, owner, level, whole * CR : whole * CR + RG, g * rest : (g + 1) * rest
+                    ]
+
+    SR = CR // PIECES
+
+    def rows_of(j):
+        return pl.ds(j * SR, SR)
+
+    def forward(p, j):
+        part = xh.at[p, c, rows_of(j)]
+        return remote(part, part, f_send.at[p, j], f_recv.at[p, j], sec, partner)
+
+    def z_copy(p, j):
+        return remote(
+            zbuf.at[p, rows_of(j)], xh.at[p, c, rows_of(j)], z_send.at[p, j], z_recv.at[p, j],
+            sec + 1, t,
+        )
 
     def r_copy(p):
         return remote(psend.at[p], precv.at[p], r_send.at[p], r_recv.at[p], sec, partner)
 
-    def x_copy(p, k):
-        return remote(
-            xs.at[p, x], xs.at[p, x], x_send.at[p, k], x_recv.at[p, k],
+    def x_copy(p, k, j):
+        part = xs.at[p, x, rows_of(j)]
+        return remote(
+            part, part, x_send.at[p, k, j], x_recv.at[p, k, j],
             sec, lax.rem(x + k, X) * 2 + c,
         )
 
@@ -183,7 +214,7 @@
         for q in range(nseq):
             rows = slice(q * SEQ, (q + 1) * SEQ)
             index = p * nseq + q
-            job = jobs[entry[p // CPB], lax.rem(index, CPB * nseq)]
+            job = jobs[entry[p // CPB], lax.rem(index, CPB * nseq), 0]
             codes = jnp.where(column_job == job, qkv[rows, 3 * COL :], 0.0).astype(BF16)
             mid = LR // 2
             query = (
@@ -212,27 +243,35 @@
                 heads[rows, cols] = jnp.dot(
                     probs, values[:, cols], preferred_element_type=F32
                 ).astype(BF16)
+
+    def project(p):
         psend[p] = jnp.dot(heads[...], obuf[1 - c], preferred_element_type=F32).astype(BF16)
         r_copy(p).start()
+
+    def project_own():
         pown[...] = jnp.dot(heads[...], obuf[c], preferred_element_type=F32)
 
     def reduce_pair(p):
         r_copy(p).wait_recv()
-        xs[p, x] = (pown[...] + precv[p].astype(F32)).astype(BF16)
-        for k in range(1, X):
-            x_copy(p, k).start()
+        for j in range(PIECES):
+            part = slice(j * SR, (j + 1) * SR)
+            xs[p, x, part] = (pown[part] + precv[p, part].astype(F32)).astype(BF16)
+            for k in range(1, X):
+                x_copy(p, k, j).start()
 
     def finish(p):
-        for k in range(1, X):
-            x_copy(p, k).wait_recv()
-        total = xs[p, 0].astype(F32)
-        for k in range(1, X):
-            total = total + xs[p, k].astype(F32)
-        zbuf[p] = (xh[p, c].astype(F32) + total).astype(BF16)
-
-        @pl.when(sec < S - 1)
-        def _():
-            z_copy(p).start()
+        for j in range(PIECES):
+            part = slice(j * SR, (j + 1) * SR)
+            for k in range(1, X):
+                x_copy(p, k, j).wait_recv()
+            total = xs[p, 0, part].astype(F32)
+            for k in range(1, X):
+                total = total + xs[p, k, part].astype(F32)
+            zbuf[p, part] = (xh[p, c, part].astype(F32) + total).astype(BF16)
+
+            @pl.when(sec < S - 1)
+            def _():
+                z_copy(p, j).start()
 
         @pl.when(sec == S - 1)
         def _():
@@ -258,7 +297,6 @@
     @pl.when(sec == 0)
     def _():
         gather_a(0)
-        gather_b(0)
 
     for k in range(1, X):
         d_peer(k).wait_recv()
@@ -272,39 +310,42 @@
     def body(p, carry):
         @pl.when(sec == 0)
         def _():
-            @pl.when(p + 1 < C)
+            gather_c(p)
+
+        @pl.when(sec > 0)
+        def _():
+            @pl.when(p == 0)
             def _():
-                gather_a(p + 1)
-
-            gather_c(p)
-
-        @pl.when(sec > 0)
-        def _():
-            z_copy(p).wait_recv()
-            forward(p).start()
+                for j in range(PIECES):
+                    z_copy(p, j).wait_recv()
+                    forward(p, j).start()
+
+            for j in range(PIECES):
+                forward(p, j).wait_recv()
+
+        front(p)
+        project(p)
+
+        @pl.when(jnp.logical_and(sec == 0, p + 1 < C))
+        def _():
+            gather_a(p + 1)
+
+        project_own()
 
         @pl.when(p > 0)
         def _():
-            reduce_pair(p - 1)
-
-        @pl.when(sec > 0)
-        def _():
-            forward(p).wait_recv()
-
-        front(p)
-
-        @pl.when(jnp.logical_and(sec == 0, p + 1 < C))
-        def _():
-            gather_b(p + 1)
-
-        @pl.when(p > 0)
-        def _():
             finish(p - 1)
 
+        @pl.when(jnp.logical_and(sec > 0, p + 1 < C))
+        def _():
+            for j in range(PIECES):
+                z_copy(p + 1, j).wait_recv()
+                forward(p + 1, j).start()
+
+        reduce_pair(p)
         return carry
 
     lax.fori_loop(0, C, body, 0)
-    reduce_pair(C - 1)
     finish(C - 1)
 
     is_local = jnp.logical_and(sec == S - 1, c == 1)
@@ -317,23 +358,25 @@
         out_ref[p] = orecv[p]
         r_copy(p).wait_send()
         for k in range(1, X):
-            x_copy(p, k).wait_send()
+            for j in range(PIECES):
+                x_copy(p, k, j).wait_send()
 
         @pl.when(sec > 0)
         def _():
-            in_copy(p, sec).wait_send()
-            forward(p).wait_send()
+            for j in range(PIECES):
+                forward(p, j).wait_send()
 
         @pl.when(sec == 0)
         def _():
-            pp_copy(p, 0).wait_send()
+            for k in range(X):
+                pp_copy(p, k).wait_send()
             for k in range(1, X):
-                px_copy(p, k).wait_send()
-                pp_copy(p, k).wait_send()
+                in_copy(p, k, sec).wait_send()
 
         @pl.when(sec < S - 1)
         def _():
-            z_copy(p).wait_send()
+            for j in range(PIECES):
+                z_copy(p, j).wait_send()
 
         @pl.when(sec == S - 1)
         def _():
@@ -348,6 +391,13 @@
         return carry
 
     lax.fori_loop(0, C, drain, 0)
+
+    @pl.when(sec > 0)
+    def _():
+        for p in range(max(0, C - IN_FLIGHT), C):
+            for k in range(X):
+                in_copy(p, k, sec).wait_send()
+
     d_own().wait_send()
     for k in range(1, X):
         d_peer(k).wait_send()
@@ -365,6 +415,9 @@
         CPB = nseq // SEQS_PER_CHUNK
         C = batches * CPB
         X, H = T // 2, F // 2
+        whole, rest, groups = packing(W)
+        packed = whole * CR + (CR // groups if rest else 0)
+        lanes = 128 if whole or groups > 1 else rest
         vmem = pl.BlockSpec(memory_space=pltpu.VMEM)
         smem = pl.BlockSpec(memory_space=pltpu.SMEM)
         anym = pl.BlockSpec(memory_space=pl.ANY)
@@ -377,8 +430,8 @@
             scratch_shapes=[
                 pltpu.VMEM((F, 3 * COL + LR), BF16),
                 pltpu.VMEM((2, COL, H), BF16),
-                pltpu.VMEM((C, CR, W), BF16),
-                pltpu.VMEM((C, T, S, CR, W), BF16),
+                pltpu.VMEM((C, packed, lanes), BF16),
+                pltpu.VMEM((C, T, S, packed, lanes), BF16),
                 pltpu.VMEM((C, 2, CR, H), BF16),
                 pltpu.VMEM((CR, F), BF16),
                 pltpu.VMEM((CR, 3 * COL + LR), F32),
@@ -392,20 +445,19 @@
                 pltpu.VMEM((C, CR, W), BF16),
                 dma((5,)),
                 dma((2 * X,)), dma((2 * X,)),
-                dma((C,)), dma((C, S)),
+                dma((C, X)), dma((C, X, S)),
                 dma((C, X)), dma((C, X)),
-                dma((C, X)), dma((C, X)),
+                dma((C, PIECES)), dma((C, PIECES)),
                 dma((C,)), dma((C,)),
-                dma((C,)), dma((C,)),
-                dma((C, X)), dma((C, X)),
-                dma((C,)), dma((C,)),
+                dma((C, X, PIECES)), dma((C, X, PIECES)),
+                dma((C, PIECES)), dma((C, PIECES)),
                 dma((C, S)), dma((C,)),
             ],
             compiler_params=pltpu.CompilerParams(
                 collective_id=0, has_side_effects=True, vmem_limit_bytes=60 * 1024 * 1024
             ),
         )(
-            entry_sequence, sequence_jobs[:, :, 0], inputs.reshape(batches, nseq * seq, W),
+            entry_sequence, sequence_jobs, inputs.reshape(batches, nseq * seq, W),
             gain, wq, wk, wv, wo, down, up,
         )
         return out.reshape(batches, nseq, seq, W)

time: 147 us -> 137 us (0.932)
  Pallas kernels: 144 us -> 133 us
    pallas_call x1, Pallas kernels: 144 us -> 133 us  [shards(): pl.pallas_call(functools.partial(kernel, S, T, C, CPB, CR, seq, F, COL, W...]
    unnamed x1 -> x2, local copies, waits for them, and re-layouts: 1.67 us -> 3.03 us
where the time goes in v2:
time: 137 us
  Pallas kernels  133 us (97%)
  local copies, waits for them, and re-layouts  3.03 us (2%)
    pallas_call x1, Pallas kernels, shards(): pl.pallas_call(functools.partial(kernel, S, T, C, CPB, CR, seq, F, COL, W...  133 us
    unnamed x2, local copies, waits for them, and re-layouts  3.03 us

profile of v2, /device:TPU:0, one launch (start us, length us, event | category | flops | bytes accessed | tf_op | source)
XLA Modules:
  0.0 136.5 jit_solution(7908580823982623829)
XLA Ops:
  0.0 1.4 copy.11.jobs
  1.4 133.5 %shard_map.100 = bf16[8,64,160]{2,1,0:T(8,128)(2,1)} custom-call(s32[4]{0:T(128)} %entry.1, s32[4,2,1]{2,1,0:T(2,128)} %copy.11.jobs, bf16[4,128,160]{2,1,0:T(8,128)(2,1)} %bitcast.3, f32[1,2560]{1,0:T(1,128)} %gain_ref.1, bf16[1,2560,640]{2,1,0:T(8,128)(2,1)} %wq.1, bf16[1,2560,640]{2,1,0:T(8,128)(2,1)} %wk.1, bf16[1,2560,640]{2,1,0:T(8,128)(2,1)} %wv.1, ...), custom_call_target="tpu_custom_call" | custom-call | tf_op jit(solution)/shard_map/pallas_call | solution.py:425
  134.9 1.7 %copy.13 = bf16[4,2,64,160]{3,2,1,0:T(8,128)(2,1)} copy(bf16[4,2,64,160]{3,2,1,0:T(8,128)(2,1)} %bitcast.2) | data formatting | bytes 327680
